TPU v7x, 32 devices: a whole 2x2x4 slice. The times are simulated.
32 devices in a mesh: wave: 8 (over y, x, core), lev: 4 (over z).
Axes of the slice: x: 2, y: 2, z: 4, core: 2. Of those that a mesh axis runs over, the one named last changes fastest.
Arguments:
- spec: bfloat16 [16, 128, 640], P('wave', 'lev'), may hold values from -1.5 to 1.5
- legendre: bfloat16 [16, 1280, 640], P('wave'), may hold values from -0.25 to 0.25
- layer_depth_share: float32 [16], P('lev'), may hold values from 0.5 to 2
- quad_weight: float32 [1280], replicated, may hold values from 8 to 32
- wave_of_slot: int32 [16], P('wave'), may hold values from 0 to 639, as said below
Outputs:
- tendency: bfloat16 [16, 128, 640], P('wave', 'lev')
Inputs may be any that keep to these rules, and one draw needn't show every extreme that they name: `wave_of_slot`: slots 2 i and 2 i + 1 hold wavenumbers m and 639 - m; no wavenumber appears twice.
All inputs are finite; a program needn't handle non-finite values.
Results may differ from a plain program's by a relative error of at most 0.0047.
The roundings to bfloat16 on the way count: a program that leaves them out, or rounds other values in their place, can miss the bound.
Values may be sent and summed in bfloat16 or wider, within the bound.
No kernel may reach another device: no remote copies, remote signals or barrier semaphores. Data moves between devices by JAX's collectives and lax.ppermute only.
A program may use at most 128 MiB of HBM per device.

v0:
```python
import math

import numpy as np
import jax
import jax.numpy as jnp
from jax import lax
from jax.experimental import pallas as pl
from jax.experimental.pallas import tpu as pltpu
from jax.sharding import PartitionSpec as P

bf16 = jnp.bfloat16
f32 = jnp.float32
FIELDS = 4
IMAGES = 4
LANES = 128
ROUNDER = 12582912.0
CHUNK = 256
GROUP = 4


def nt(a, b):
    return lax.dot_general(a, b, (((1,), (1,)), ((), ())), preferred_element_type=f32)


def nn(a, b):
    return lax.dot_general(a, b, (((1,), (0,)), ((), ())), preferred_element_type=f32)


def circle_polynomials():
    f = np.cos(np.pi * (np.arange(4000) + 0.5) / 8000) * 0.5
    z = f * f
    out = []
    for values, degree in ((np.cos(2 * np.pi * f), 6), (np.sin(2 * np.pi * f) / f, 6)):
        fit = np.polynomial.chebyshev.Chebyshev.fit(z, values, degree, domain=[0, 0.25])
        out.append([float(c) for c in fit.convert(kind=np.polynomial.Polynomial).coef])
    return out


COS_POLY, SIN_POLY = circle_polynomials()


def horner(z, coefs):
    acc = jnp.full_like(z, coefs[-1])
    for c in coefs[-2::-1]:
        acc = acc * z + c
    return acc


def cos_sin(count, length, inverse):
    turns = (count * inverse + ROUNDER) - ROUNDER
    f = (count - turns * length) * inverse
    z = f * f
    return horner(z, COS_POLY), f * horner(z, SIN_POLY)


def image_signs():
    return np.array([[1, 1, 1, 1], [-1, 1, -1, 1], [1, 1, -1, -1], [-1, 1, 1, -1]], np.float32)


class Sizes:
    def __init__(self, n_wave, n_lev, slots, cols, lats, span, layers):
        self.n_wave, self.n_lev, self.slots, self.cols = n_wave, n_lev, slots, cols
        self.lats, self.span, self.layers = lats, span, layers
        self.rows = lats // n_wave // 2
        self.half = self.rows // 2
        self.circles = lats // 2
        self.points = self.circles + 11
        self.width = -(-self.points // CHUNK) * CHUNK
        self.tiles = self.width // LANES
        self.sent = self.rows + 8
        self.keys = 8 * n_wave

    def fits(self):
        return (
            self.slots == 2
            and self.cols == 32
            and self.layers == 4
            and self.n_wave == 8
            and self.rows % 16 == 0
            and self.half % (2 * GROUP) == 0
            and self.half % 8 == 0
            and self.half * 4 * self.n_wave == self.lats
            and self.span % LANES == 0
            and (self.n_wave * self.rows) % LANES == 0
            and self.tiles <= 8
        )

    def block_starts(self, owner):
        h = self.half
        return (
            (h * owner, self.circles - h * (owner + 1)),
            (self.lats - h * (owner + 1), self.circles + h * owner),
        )


def spread_matrix(n):
    signs = image_signs()
    out = np.zeros((LANES, 4 * LANES), np.float32)
    for p in range(4):
        for hemi in range(2):
            for field in range(FIELDS):
                for layer in range(n.layers):
                    src = p * 32 + hemi * 16 + field * 4 + layer
                    for image in range(IMAGES):
                        out[src, p * LANES + image * 32 + field * 8 + hemi * 4 + layer] = signs[p, image]
    return out


def order_matrix(n):
    out = np.zeros((LANES, LANES), np.float32)
    for parity in range(2):
        for part in range(2):
            for hemi in range(2):
                for field in range(FIELDS):
                    for layer in range(n.layers):
                        row = hemi * 64 + parity * 32 + part * 16 + field * 4 + layer
                        lane = (parity * 2 + part) * 32 + field * 8 + hemi * 4 + layer
                        out[row, lane] = 1.0
    return out


def live_spec(n, spec, wave):
    degree = lax.broadcasted_iota(jnp.int32, (n.cols, n.span), 1)
    live = degree < n.span - wave
    return jnp.where(live, spec.astype(f32), 0.0), live


def layer_sums(n, masked, share_ref):
    row = lax.broadcasted_iota(jnp.int32, (n.cols, n.span), 0)
    layer = row % n.layers
    weight = jnp.where(
        layer < 2,
        jnp.where(layer == 0, share_ref[0], share_ref[1]),
        jnp.where(layer == 2, share_ref[2], share_ref[3]),
    )
    warm = (row // n.layers) % FIELDS == FIELDS - 1
    y = jnp.where(warm, masked * weight, 0.0)
    y = y + pltpu.roll(y, n.cols - 1, 0)
    return y + pltpu.roll(y, n.cols - 2, 0)


def fetch(pairs, sems):
    copies = [pltpu.make_async_copy(src, dst, sems.at[k]) for k, (src, dst) in enumerate(pairs)]
    for copy in copies:
        copy.start()
    return copies


def forward_kernel(n, wave_hbm, share_hbm, spec_hbm, leg_hbm, out_ref, total_hbm, wave_ref, share_ref, spec_ref, leg, total_ref, acc, sems, leg_sems, done_sem):
    small = fetch(((wave_hbm, wave_ref), (share_hbm, share_ref), (spec_hbm, spec_ref)), sems)
    halves = [(s, hemi) for s in range(2) for hemi in range(2)]
    big = fetch(
        [
            (leg_hbm.at[s, pl.ds(hemi * n.circles, n.circles), :], leg.at[s, pl.ds(hemi * n.circles, n.circles), :])
            for s, hemi in halves
        ],
        leg_sems,
    )
    for copy in small:
        copy.wait()
    tables = []
    for s in range(2):
        masked, _ = live_spec(n, spec_ref[s], wave_ref[s])
        sums = layer_sums(n, masked, share_ref)
        for part in range(2):
            total_ref[2 * s + part : 2 * s + part + 1, :] = sums[part * 16 + 12 : part * 16 + 13, :]
        scaled = masked * jnp.where(wave_ref[s] == 0, 1.0, 2.0)
        none = jnp.zeros_like(scaled[:16])
        for hemi in range(2):
            rows = []
            for parity in range(2):
                mine = wave_ref[s] % 2 == parity
                for part in range(2):
                    chunk = jnp.where(mine, scaled[part * 16 : part * 16 + 16], 0.0)
                    rows += [chunk, none] if hemi == 0 else [none, chunk]
            tables.append(jnp.concatenate(rows, 0).astype(bf16))
    totals_out = pltpu.make_async_copy(total_ref, total_hbm, done_sem)
    totals_out.start()
    for k, (s, hemi) in enumerate(halves):
        big[k].wait()
        piece = nt(leg[s, hemi * n.circles : (hemi + 1) * n.circles, :], tables[k])
        acc[hemi] = piece if s == 0 else acc[hemi] + piece
    even = jnp.where(wave_ref[0] % 2 == 0, wave_ref[0], wave_ref[1])
    lane = lax.broadcasted_iota(jnp.int32, (8, LANES), 1)
    tag = jnp.where(lane < LANES // 2, even // 16, even % 16).astype(f32)
    for owner in range(n.n_wave):
        starts = n.block_starts(owner)
        for b in range(2):
            north = acc[0, starts[0][b] : starts[0][b] + n.half, :]
            south = acc[1, starts[1][b] - n.circles : starts[1][b] - n.circles + n.half, :]
            out_ref[owner, b * n.half : (b + 1) * n.half, :] = (north + south).astype(bf16)
        out_ref[owner, n.rows : n.sent, :] = tag.astype(bf16)
    totals_out.wait()


def grid_kernel(n, got_ref, spread_ref, sign_ref, cor_ref, inv_ref, quad_ref, out_ref, spread, table_a, table_b, coef_a, coef_b, ret, rows):
    device = lax.axis_index("wave")
    first_circle = device * n.half
    top = n.span - 1
    for p in range(4):
        spread[p] = nn(got_ref[...], spread_ref[:, p * LANES : (p + 1) * LANES])
    lane = lax.broadcasted_iota(jnp.int32, (8, LANES), 1)
    lane_f = lane.astype(f32)
    north = (lane // 4) % 2 == 0
    raw = got_rows_f32(n, got_ref)
    tag = jnp.where(lane < LANES // 2, raw * 16.0, raw)
    even_m = tag + pltpu.roll(tag, LANES // 2, 1)
    odd_m = float(top) - even_m

    def sizes(i):
        short = first_circle + i
        return short, n.circles - 1 - short

    def build(i, u, table):
        short, long = sizes(i)
        cut = (short + 6).astype(f32)
        len_s = (20 + 4 * short).astype(f32)
        len_l = (20 + 4 * long).astype(f32)
        inv_s = inv_ref[short]
        inv_l = inv_ref[long]

        def places(point):
            own = point < cut
            return own, jnp.where(own, point, point - cut), jnp.where(own, len_s, len_l), jnp.where(own, inv_s, inv_l)

        tile = lax.broadcasted_iota(jnp.int32, (8, LANES), 0)
        _, j, length, inverse = places((tile * LANES + lane).astype(f32))
        top_c, top_s = cos_sin(j * float(top), length, inverse)
        for t in range(n.tiles):
            own, j, length, inverse = places(lane_f + float(t * LANES))
            c, s = cos_sin(even_m * j, length, inverse)
            tc = jnp.broadcast_to(top_c[t : t + 1, :], (8, LANES))
            ts = jnp.broadcast_to(top_s[t : t + 1, :], (8, LANES))
            odd_c = tc * c + ts * s
            odd_s = ts * c - tc * s
            both = jnp.concatenate([c, s, odd_c, odd_s], 0)
            own = jnp.concatenate([own] * 4, 0)
            two = jnp.concatenate([jnp.where(own, both, 0.0), jnp.where(own, 0.0, both)], 0)
            table[u, :, t * LANES : (t + 1) * LANES] = two.astype(bf16)

    def gather(i, u, coef):
        short, long = sizes(i)
        parts = []
        for circle, row_n, row_s in (
            (short, i, n.half - 1 - i),
            (long, n.rows - 1 - i, n.half + i),
        ):
            length = (20 + 4 * circle).astype(f32)
            even_ok = 2.0 * even_m < length
            odd_ok = 2.0 * odd_m < length
            for p in range(4):
                up = spread[p, pl.ds(row_n, 8, stride=n.sent), :]
                down = spread[p, pl.ds(row_s, 8, stride=n.sent), :]
                parts.append(jnp.where(odd_ok if p > 1 else even_ok, jnp.where(north, up, down), 0.0))
        coef[u] = jnp.transpose(jnp.concatenate(parts, 0)).astype(bf16)

    south = lax.broadcasted_iota(jnp.int32, (8, n.width), 0) // 4
    point = lax.broadcasted_iota(jnp.int32, (8, n.width), 1)
    point_row = lax.broadcasted_iota(jnp.int32, (1, n.width), 1)
    signs = [sign_ref[p : p + 1, :] for p in range(4)]
    group = lane // 32
    kinetic = jnp.where((lane // 8) % FIELDS == 2, 0.5, 1.0)

    def transform(i, u, table, coef):
        short, long = sizes(i)
        cut = short + 6
        tab = table[u]
        grid = nn(coef[u], tab).reshape(IMAGES, FIELDS, 8, n.width)
        spin = jnp.where(point < cut, cor_ref[short], cor_ref[long])
        spin = jnp.where(south == 0, spin, -spin)
        x, y, curl, warm = grid[:, 0], grid[:, 1], grid[:, 2], grid[:, 3]
        absolute = curl + spin
        prods = jnp.stack([absolute * x, absolute * y, x * x + y * y, x * warm], 1)
        prods = prods.reshape(LANES, n.width).astype(bf16)
        edge = (point_row == 0) | (point_row == cut - 1) | (point_row == cut) | (point_row == n.points - 1)
        share = jnp.where(edge, 0.5, jnp.where(point_row < n.points, 1.0, 0.0)).astype(bf16)
        total = nt(tab * share, prods)
        for k, circle in enumerate((short, long)):
            length = (20 + 4 * circle).astype(f32)
            even_ok = 2.0 * even_m < length
            odd_ok = 2.0 * odd_m < length
            folded = None
            for p in range(4):
                y = total[(4 * k + p) * 8 : (4 * k + p + 1) * 8] * signs[p]
                y = y + pltpu.roll(y, 64, 1)
                y = y + pltpu.roll(y, 32, 1)
                y = jnp.where(odd_ok if p > 1 else even_ok, y, 0.0)
                folded = y if folded is None else jnp.where(group == p, y, folded)
            weight = jnp.where(north, quad_ref[circle], quad_ref[n.lats - 1 - circle]) * (inv_ref[circle] * kinetic)
            ret[k, i] = folded * weight

    def ready(start, table, coef):
        for u in range(GROUP):
            i = jnp.minimum(start + u, n.half - 1)
            build(i, u, table)
            gather(i, u, coef)

    def work(start, table, coef):
        for u in range(GROUP):
            transform(start + u, u, table, coef)

    def step(k, carry):
        start = 2 * GROUP * k
        ready(start + GROUP, table_b, coef_b)
        work(start, table_a, coef_a)
        ready(start + 2 * GROUP, table_a, coef_a)
        work(start + GROUP, table_b, coef_b)
        return carry

    ready(0, table_a, coef_a)
    lax.fori_loop(0, n.half // (2 * GROUP), step, 0)

    def place(i, carry):
        other = n.half - 1 - i
        rows[pl.ds(i, 8, stride=n.rows), :] = jnp.where(north, ret[0, i], ret[0, other])
        rows[pl.ds(n.half + i, 8, stride=n.rows), :] = jnp.where(north, ret[1, other], ret[1, i])
        return carry

    lax.fori_loop(0, n.half, place, 0, unroll=4)
    out_ref[...] = rows[...].astype(bf16)


def got_rows_f32(n, got_ref):
    pieces = [got_ref[src * n.sent + n.rows : src * n.sent + n.rows + 8, :].astype(f32)[:1] for src in range(n.n_wave)]
    return jnp.concatenate(pieces, 0)


def back_kernel(n, wave_hbm, share_hbm, *refs):
    deeper_hbm = refs[: n.n_lev - 1]
    spec_ref, back_ref, order_ref, leg, out_ref, wave_ref, share_ref, deeper_ref, turn, sems = refs[n.n_lev - 1 :]
    copies = fetch(
        [(wave_hbm, wave_ref), (share_hbm, share_ref)] + [(ref, deeper_ref.at[k]) for k, ref in enumerate(deeper_hbm)],
        sems,
    )
    for owner in range(n.n_wave):
        starts = n.block_starts(owner)
        for b in range(2):
            block = back_ref[owner * n.rows + b * n.half : owner * n.rows + (b + 1) * n.half, :]
            for hemi in range(2):
                at = starts[hemi][b] - hemi * n.circles
                turn[hemi, at : at + n.half, :] = block
    turned = [nt(order_ref[hemi * 64 : hemi * 64 + 64, :], turn[hemi]) for hemi in range(2)]
    row = lax.broadcasted_iota(jnp.int32, (n.cols, n.span), 0)
    target = (row // n.layers) % FIELDS == 2
    for copy in copies:
        copy.wait()
    deeper = None
    for k in range(n.n_lev - 1):
        deeper = deeper_ref[k] if deeper is None else deeper + deeper_ref[k]
    for s in range(2):
        masked, live = live_spec(n, spec_ref[s], wave_ref[s])
        high = pltpu.roll(layer_sums(n, masked, share_ref), n.cols - n.layers, 0)
        if deeper is not None:
            low = jnp.where(row < 16, deeper[2 * s : 2 * s + 1], deeper[2 * s + 1 : 2 * s + 2])
            high = high + low
        even = wave_ref[s] % 2 == 0
        tendency = jnp.where(target, high, 0.0)
        for hemi in range(2):
            mine = jnp.where(even, turned[hemi][:32], turned[hemi][32:])
            tendency = tendency + nn(mine.astype(bf16), leg[s, hemi * n.circles : (hemi + 1) * n.circles, :])
        out_ref[s] = jnp.where(live, tendency, 0.0).astype(bf16)


def smem():
    return pl.BlockSpec(memory_space=pltpu.SMEM)


def vmem():
    return pl.BlockSpec(memory_space=pltpu.VMEM)


def hbm():
    return pl.BlockSpec(memory_space=pltpu.HBM)


def grid_call(n, got, quad_weight):
    params = pltpu.CompilerParams(vmem_limit_bytes=24 * 1024 * 1024)
    all_rows = n.n_wave * n.rows
    circle = np.arange(n.circles)
    spin = (2.0 * np.cos((circle + 0.5) * (math.pi / n.lats))).astype(np.float32)
    inverse = (1.0 / (20 + 4 * circle)).astype(np.float32)
    signs = np.zeros((8, LANES), np.float32)
    signs[:4] = np.repeat(image_signs(), LANES // IMAGES, axis=1)
    return pl.pallas_call(
        lambda *refs: grid_kernel(n, *refs),
        out_shape=jax.ShapeDtypeStruct((all_rows, LANES), bf16),
        in_specs=[vmem(), vmem(), vmem(), smem(), smem(), smem()],
        out_specs=vmem(),
        scratch_shapes=[
            pltpu.VMEM((4, n.n_wave * n.sent, LANES), f32),
            pltpu.VMEM((GROUP, n.keys, n.width), bf16),
            pltpu.VMEM((GROUP, n.keys, n.width), bf16),
            pltpu.VMEM((GROUP, LANES, n.keys), bf16),
            pltpu.VMEM((GROUP, LANES, n.keys), bf16),
            pltpu.VMEM((2, n.half, 8, LANES), f32),
            pltpu.VMEM((all_rows, LANES), f32),
        ],
        compiler_params=params,
        name="grid_stage",
    )(
        got,
        jnp.asarray(spread_matrix(n), bf16),
        jnp.asarray(signs),
        jnp.asarray(spin),
        jnp.asarray(inverse),
        quad_weight,
    )


def fast_body(n, spec, legendre, layer_depth_share, quad_weight, wave_of_slot):
    params = pltpu.CompilerParams(vmem_limit_bytes=24 * 1024 * 1024)
    all_rows = n.n_wave * n.rows
    dma = pltpu.SemaphoreType.DMA
    small = [pltpu.SMEM((2,), jnp.int32), pltpu.SMEM((n.layers,), f32)]
    sent, totals = pl.pallas_call(
        lambda *refs: forward_kernel(n, *refs),
        out_shape=(
            jax.ShapeDtypeStruct((n.n_wave, n.sent, LANES), bf16),
            jax.ShapeDtypeStruct((4, n.span), f32),
        ),
        in_specs=[hbm()] * 4,
        out_specs=(vmem(), hbm()),
        scratch_shapes=small
        + [
            pltpu.VMEM(spec.shape, bf16),
            pltpu.VMEM(legendre.shape, bf16),
            pltpu.VMEM((4, n.span), f32),
            pltpu.VMEM((2, n.circles, LANES), f32),
            dma((3,)),
            dma((4,)),
            dma,
        ],
        compiler_params=params,
        name="legendre_forward",
    )(wave_of_slot, layer_depth_share, spec, legendre)
    deeper = [
        lax.ppermute(totals, "lev", [(i, i - hop) for i in range(hop, n.n_lev)]) for hop in range(1, n.n_lev)
    ]
    got = lax.all_to_all(sent, "wave", split_axis=0, concat_axis=0, tiled=True)
    out = grid_call(n, got.reshape(n.n_wave * n.sent, LANES), quad_weight)
    back = lax.all_to_all(
        out.reshape(n.n_wave, n.rows, LANES), "wave", split_axis=0, concat_axis=0, tiled=True
    )
    return pl.pallas_call(
        lambda *refs: back_kernel(n, *refs),
        out_shape=jax.ShapeDtypeStruct(spec.shape, bf16),
        in_specs=[hbm()] * (n.n_lev + 1) + [vmem()] * 4,
        out_specs=vmem(),
        scratch_shapes=small
        + [
            pltpu.VMEM((max(n.n_lev - 1, 1), 4, n.span), f32),
            pltpu.VMEM((2, n.circles, LANES), bf16),
            dma((n.n_lev + 1,)),
        ],
        compiler_params=params,
        name="legendre_back",
    )(
        wave_of_slot,
        layer_depth_share,
        *deeper,
        spec,
        back.reshape(all_rows, LANES),
        jnp.asarray(order_matrix(n), bf16),
        legendre,
    )


full_turn = 2.0 * math.pi


def carried_in(part, axis, combine, identity):
    count = lax.axis_size(axis)
    place = lax.axis_index(axis)
    ahead = count - 1 - place
    gathered = lax.all_gather(part, axis)
    state = jnp.zeros_like(part) + jnp.asarray(identity, part.dtype)

    def one(hop, state):
        source = count - 1 - hop
        return combine(state, lax.dynamic_index_in_dim(gathered, source, 0, False))

    return lax.fori_loop(0, ahead, one, state)


def rate_bundle(
    eastward_velocity,
    northward_velocity,
    local_curl_spin,
    thermal_state,
    planetary_rotation_effect,
    processor_dimension,
):
    absolute = local_curl_spin + planetary_rotation_effect
    return jnp.stack(
        [
            absolute * eastward_velocity,
            absolute * northward_velocity,
            0.5 * (eastward_velocity * eastward_velocity + northward_velocity * northward_velocity),
            eastward_velocity * thermal_state,
        ],
        axis=processor_dimension,
    )


def row_latitudes(device, per_dev, total_lat):
    row_ids = jnp.arange(per_dev, dtype=jnp.int32)
    quarter = per_dev // 4
    block_ids = row_ids // 4
    hemisphere = row_ids // 2 % 2
    member = row_ids % 2
    first_dist = device * quarter + block_ids
    pole_dist = jnp.where(member == 0, first_dist, total_lat // 2 - 1 - first_dist)
    return jnp.where(hemisphere == 0, pole_dist, total_lat - 1 - pole_dist)


def add_terms(earlier, later):
    return earlier + later


def general_body(spec, legendre, layer_depth_share, quad_weight, wave_of_slot):
    number_of_slots, columns, degree_list = spec.shape
    total_lat = legendre.shape[1]
    groups = lax.axis_size("wave")
    device = lax.axis_index("wave")
    per_dev = total_lat // groups
    layers_on_processor = layer_depth_share.shape[0]
    field_stack = columns // (2 * layers_on_processor)
    flat_rows = field_stack * layers_on_processor
    max_points = 20 + 4 * (total_lat // 2 - 1)
    all_waves = lax.all_gather(wave_of_slot, "wave", axis=0, tiled=True)
    wave_count = all_waves.shape[0]
    weight_two = jnp.where(all_waves == 0, 1.0, 2.0).astype(jnp.float32)
    degree_index = jnp.arange(degree_list, dtype=jnp.int32)
    valid_cols = degree_index[None, :] < (degree_list - wave_of_slot)[:, None]
    screened_entries = jnp.where(valid_cols[:, None, :], spec, jnp.zeros_like(spec))
    thermal_state = screened_entries.reshape(
        number_of_slots, 2, field_stack, layers_on_processor, degree_list
    )[:, :, 3].astype(jnp.float32)
    scaled_entries = thermal_state * layer_depth_share[None, None, :, None]
    below_sum = jnp.flip(jnp.cumsum(jnp.flip(scaled_entries, 2), 2), 2)
    deeper = carried_in(
        below_sum[:, :, 0],
        "lev",
        add_terms,
        jnp.zeros((number_of_slots, 2, degree_list), jnp.float32),
    )
    geopot = below_sum + deeper[:, :, None, :]
    fourier = jnp.einsum(
        "sln,scn->lsc", legendre, screened_entries, preferred_element_type=jnp.float32
    ).astype(jnp.bfloat16)
    send_order = row_latitudes(
        jnp.arange(groups, dtype=jnp.int32)[:, None], per_dev, total_lat
    ).reshape(-1)
    send_rows = jnp.take(fourier, send_order, axis=0).reshape(total_lat, number_of_slots * columns)
    received = lax.all_to_all(send_rows, "wave", split_axis=0, concat_axis=1, tiled=True)
    coeffs = received.reshape(per_dev, wave_count, 2, flat_rows)
    latitudes = row_latitudes(device, per_dev, total_lat)
    lengths = 20 + 4 * jnp.minimum(latitudes, total_lat - 1 - latitudes)
    planetary_rotation_effect = 2.0 * jnp.cos(
        (latitudes.astype(jnp.float32) + 0.5) * (math.pi / total_lat)
    )
    row_scale = quad_weight[latitudes] / lengths.astype(jnp.float32)
    quarter = per_dev // 4
    pair_points = max_points + 20
    tile_count = -(-pair_points // 128)
    padded = tile_count * 128
    pair_len = lengths.reshape(quarter, 2, 2)[:, 0, :]
    first_len = pair_len[:, 0:1]
    second_len = pair_len[:, 1:2]
    points = jnp.arange(padded, dtype=jnp.int32)[None, :]
    first_lat = points < first_len
    in_pair = points < pair_points
    local_idx = jnp.where(first_lat, points, points - first_len)
    point_len = jnp.where(first_lat, first_len, second_len)
    phase_int = all_waves[None, :, None] * local_idx[:, None, :] % point_len[:, None, :]
    angles = phase_int.astype(jnp.float32) * full_turn / point_len.astype(jnp.float32)[:, None, :]
    cosine = jnp.cos(angles)
    sine_vals = jnp.sin(angles)
    resolved = (2 * all_waves[None, :, None] < point_len[:, None, :]) & in_pair[:, None, :]
    amplitude = jnp.where(resolved, weight_two[None, :, None], 0.0)
    forward_tab = jnp.concatenate([amplitude * cosine, -(amplitude * sine_vals)], 1).astype(
        jnp.bfloat16
    )
    back_tab = jnp.concatenate(
        [jnp.where(resolved, cosine, 0.0), -jnp.where(resolved, sine_vals, 0.0)], 1
    ).astype(jnp.bfloat16)
    forward_tiles = forward_tab.reshape(quarter, 2 * wave_count, tile_count, 128)
    back_tiles = back_tab.reshape(quarter, 2 * wave_count, tile_count, 128)
    tile_start = jnp.arange(tile_count, dtype=jnp.int32)[None, :] * 128
    owner_second = tile_start + 128 > first_len
    boundary = first_len[:, 0] // 128
    is_bound = jnp.arange(tile_count, dtype=jnp.int32)[None, :] == boundary[:, None]
    first_tiles = first_lat.reshape(quarter, tile_count, 128)
    stacked = coeffs.reshape(quarter, 2, 2, wave_count, 2, flat_rows).transpose(0, 1, 2, 4, 3, 5)
    stacked = stacked.reshape(quarter, 2, 2, 2 * wave_count, flat_rows)
    coef_tiles = jnp.where(
        owner_second[:, None, :, None, None],
        stacked[:, :, 1][:, :, None],
        stacked[:, :, 0][:, :, None],
    )
    grid_tiles = jnp.einsum(
        "qatkf,qktp->qaftp", coef_tiles, forward_tiles, preferred_element_type=jnp.float32
    )
    bound_fwd = jnp.take_along_axis(forward_tiles, boundary[:, None, None, None], axis=2)[:, :, 0]
    bound_back = jnp.take_along_axis(back_tiles, boundary[:, None, None, None], axis=2)[:, :, 0]
    edge_grid = jnp.einsum(
        "qakf,qkp->qafp", stacked[:, :, 0], bound_fwd, preferred_element_type=jnp.float32
    )
    use_edge = is_bound[:, :, None] & first_tiles
    grid_tiles = jnp.where(use_edge[:, None, None], edge_grid[:, :, :, None, :], grid_tiles)
    grid_vals = grid_tiles.reshape(quarter, 2, field_stack, layers_on_processor, padded)
    row_cor = planetary_rotation_effect.reshape(quarter, 2, 2)
    point_cor = jnp.where(first_lat[:, None, :], row_cor[:, :, 0:1], row_cor[:, :, 1:2])[
        :, :, None, :
    ]
    products = rate_bundle(
        grid_vals[:, :, 0], grid_vals[:, :, 1], grid_vals[:, :, 2], grid_vals[:, :, 3], point_cor, 2
    )
    products = products.astype(jnp.bfloat16).reshape(quarter, 2, flat_rows, tile_count, 128)
    keep = jnp.where(owner_second[:, :, None], jnp.logical_not(first_tiles), first_tiles)
    main_prods = jnp.where(keep[:, None, None], products, jnp.zeros_like(products))
    per_tile = jnp.einsum(
        "qaftp,qktp->qatkf", main_prods, back_tiles, preferred_element_type=jnp.float32
    )
    bound_prods = jnp.take_along_axis(products, boundary[:, None, None, None, None], axis=3)[
        :, :, :, 0
    ]
    bound_first = jnp.take_along_axis(first_tiles, boundary[:, None, None], axis=1)[:, 0]
    bound_prods = jnp.where(bound_first[:, None, None, :], bound_prods, jnp.zeros_like(bound_prods))
    edge_back = jnp.einsum(
        "qafp,qkp->qakf", bound_prods, bound_back, preferred_element_type=jnp.float32
    )
    owner_mask = owner_second[:, None, :, None, None]
    first_ret = jnp.sum(jnp.where(owner_mask, 0.0, per_tile), axis=2) + edge_back
    second_ret = jnp.sum(jnp.where(owner_mask, per_tile, 0.0), axis=2)
    returned = jnp.stack([first_ret, second_ret], axis=2)
    returned = (returned * row_scale.reshape(quarter, 2, 2)[:, :, :, None, None]).astype(
        jnp.bfloat16
    )
    out_rows = returned.reshape(quarter, 2, 2, 2, wave_count, flat_rows).transpose(0, 1, 2, 4, 3, 5)
    out_rows = out_rows.reshape(per_dev, wave_count * columns)
    gathered_rows = lax.all_to_all(out_rows, "wave", split_axis=1, concat_axis=0, tiled=True)
    inverse = (
        jnp.zeros((total_lat,), jnp.int32)
        .at[send_order]
        .set(jnp.arange(total_lat, dtype=jnp.int32))
    )
    back_fourier = jnp.take(gathered_rows, inverse, axis=0).reshape(
        total_lat, number_of_slots, columns
    )
    tendency = jnp.einsum(
        "lsc,sln->scn", back_fourier, legendre, preferred_element_type=jnp.float32
    )
    tendency = tendency.reshape(number_of_slots, 2, field_stack, layers_on_processor, degree_list)
    tendency = tendency.at[:, :, 2].add(geopot)
    tendency = jnp.where(valid_cols[:, None, None, None, :], tendency, 0.0)
    return tendency.reshape(number_of_slots, columns, degree_list).astype(jnp.bfloat16)


def solution(mesh):
    def body(spec, legendre, layer_depth_share, quad_weight, wave_of_slot):
        slots, cols, span = spec.shape
        layers = layer_depth_share.shape[0]
        n = Sizes(mesh.shape["wave"], mesh.shape["lev"], slots, cols, legendre.shape[1], span, layers)
        step = (lambda *args: fast_body(n, *args)) if n.fits() else general_body
        return step(spec, legendre, layer_depth_share, quad_weight, wave_of_slot)

    in_specs = (P("wave", "lev", None), P("wave", None, None), P("lev"), P(), P("wave"))
    out_specs = P("wave", "lev", None)
    return jax.shard_map(body, mesh=mesh, in_specs=in_specs, out_specs=out_specs, check_vma=False)
```

profile of v0, /device:TPU:0, one launch (start us, length us, event | category | flops | bytes accessed | tf_op | source)
XLA Modules:
  0.0 48.0 jit_solution(15850119795701298794)
XLA Ops:
  0.0 1.9 %copy-done = bf16[2,1280,640]{2,1,0:T(8,128)(2,1)S(1)} copy-done((bf16[2,1280,640]{2,1,0:T(8,128)(2,1)S(1)}, bf16[2,1280,640]{2,1,0:T(8,128)(2,1)}, u32[]{:S(2)}) %copy-start) | copy-done | bytes 3276824
  1.9 0.9 %copy-done.3 = bf16[2,32,640]{2,1,0:T(8,128)(2,1)S(1)} copy-done((bf16[2,32,640]{2,1,0:T(8,128)(2,1)S(1)}, bf16[2,32,640]{2,1,0:T(8,128)(2,1)}, u32[]{:S(2)}) %copy-start.3) | copy-done | bytes 81944
  2.8 0.7 %copy-done.17 = s32[2]{0:T(128)S(1)} copy-done((s32[2]{0:T(128)S(1)}, s32[2]{0:T(128)}, u32[]{:S(2)}) %copy-start.17) | copy-done | bytes 32
  3.5 0.7 %copy-done.19 = f32[4]{0:T(128)S(1)} copy-done((f32[4]{0:T(128)S(1)}, f32[4]{0:T(128)}, u32[]{:S(2)}) %copy-start.19) | copy-done | bytes 40
  4.2 0.0 copy-start.6
  4.2 2.6 %legendre_forward.1 = (bf16[8,88,128]{2,1,0:T(8,128)(2,1)S(1)}, f32[4,640]{1,0:T(4,128)S(1)}) custom-call(s32[2]{0:T(128)S(1)} %copy-done.17, f32[4]{0:T(128)S(1)} %copy-done.19, bf16[2,32,640]{2,1,0:T(8,128)(2,1)S(1)} %copy-done.3, bf16[2,1280,640]{2,1,0:T(8,128)(2,1)S(1)} %copy-done), custom_call_target="tpu_custom_call" | custom-call | tf_op jit(solution)/shard_map/legendre_forward/pallas_call | solution.py:415
  6.9 0.6 %copy-done.21 = f32[4,640]{1,0:T(4,128)} copy-done((f32[4,640]{1,0:T(4,128)}, f32[4,640]{1,0:T(4,128)S(1)}, u32[]{:S(2)}) %copy-start.21) | copy-done | bytes 10264
  7.4 11.0 %all_to_all.10 = bf16[8,88,128]{2,1,0:T(8,128)(2,1)S(1)} all-to-all(bf16[8,88,128]{2,1,0:T(8,128)(2,1)S(1)} %get-tuple-element.8), channel_id=1, replica_groups=mesh['wave'=8,'lev'=4] {'wave'}, dimensions={0} | all-to-all | bytes 360448 | tf_op jit(solution)/shard_map/all_to_all | solution.py:439
  18.5 10.8 %grid_stage.1 = bf16[640,128]{1,0:T(8,128)(2,1)S(1)} custom-call(bf16[704,128]{1,0:T(8,128)(2,1)S(1)} %bitcast.3, bf16[128,512]{1,0:T(8,128)(2,1)S(1)} %copy-done.5, f32[8,128]{1,0:T(8,128)S(1)} %copy-done.16, f32[640]{0:T(1024)S(1)} %copy-done.15, f32[640]{0:T(1024)S(1)} %copy-done.14, f32[1280]{0:T(1024)S(1)} %copy-done.13), custom_call_target="tpu_custom_call" | custom-call | tf_op jit(solution)/shard_map/grid_stage/pallas_call | solution.py:384
  29.3 0.7 %copy-done.2 = bf16[640,128]{1,0:T(8,128)(2,1)} copy-done((bf16[640,128]{1,0:T(8,128)(2,1)}, bf16[640,128]{1,0:T(8,128)(2,1)S(1)}, u32[]{:S(2)}) %copy-start.2) | copy-done | bytes 163864
  29.9 3.4 %all-to-all-start.1 = ((bf16[8,80,128]{2,1,0:T(8,128)(2,1)}), bf16[8,80,128]{2,1,0:T(8,128)(2,1)S(1)}, u32[]{:S(2)}, u32[]{:S(2)}) async-start(bf16[8,80,128]{2,1,0:T(8,128)(2,1)} %bitcast.5), calls=%async_computation.1 | async-start | bytes 327680 | tf_op jit(solution)/shard_map/all_to_all | solution.py:441
  33.3 1.3 %collective-permute-start.2 = (f32[4,640]{1,0:T(4,128)}, f32[4,640]{1,0:T(4,128)S(1)}, u32[]{:S(2)}, u32[]{:S(2)}) collective-permute-start(f32[4,640]{1,0:T(4,128)} %copy-done.21), channel_id=1, source_target_pairs={{3,0},{7,4},{11,8},{15,12},{19,16},{23,20},{27,24},{31,28}} | collective-permute-start | bytes 30728 | tf_op jit(solution)/shard_map/ppermute | solution.py:437
  34.6 1.3 %collective-permute-start.1 = (f32[4,640]{1,0:T(4,128)}, f32[4,640]{1,0:T(4,128)S(1)}, u32[]{:S(2)}, u32[]{:S(2)}) collective-permute-start(f32[4,640]{1,0:T(4,128)} %copy-done.21), channel_id=1, source_target_pairs={{2,0},{3,1},{6,4},{7,5},{10,8},{11,9},{14,12},{15,13},{18,16},{19,... | collective-permute-start | bytes 30728 | tf_op jit(solution)/shard_map/ppermute | solution.py:437
  35.9 1.3 %collective-permute-start = (f32[4,640]{1,0:T(4,128)}, f32[4,640]{1,0:T(4,128)S(1)}, u32[]{:S(2)}, u32[]{:S(2)}) collective-permute-start(f32[4,640]{1,0:T(4,128)} %copy-done.21), channel_id=1, source_target_pairs={{1,0},{2,1},{3,2},{5,4},{6,5},{7,6},{9,8},{10,9},{11,10},{13,12},{... | collective-permute-start | bytes 30728 | tf_op jit(solution)/shard_map/ppermute | solution.py:437
  37.2 3.7 %collective-permute-done.2.refs_4_ = f32[4,640]{1,0:T(4,128)S(1)} collective-permute-done((f32[4,640]{1,0:T(4,128)}, f32[4,640]{1,0:T(4,128)S(1)}, u32[]{:S(2)}, u32[]{:S(2)}) %collective-permute-start.2) | collective-permute-done | bytes 10272 | tf_op jit(solution)/shard_map/ppermute | solution.py:437
  40.9 0.6 %copy-done.7 = f32[4,640]{1,0:T(4,128)} copy-done((f32[4,640]{1,0:T(4,128)}, f32[4,640]{1,0:T(4,128)S(1)}, u32[]{:S(2)}) %copy-start.7) | copy-done | bytes 10264
  41.5 0.6 %copy-done.9 = f32[4,640]{1,0:T(4,128)} copy-done((f32[4,640]{1,0:T(4,128)}, f32[4,640]{1,0:T(4,128)S(1)}, u32[]{:S(2)}) %copy-start.9) | copy-done | bytes 10264
  42.1 0.6 %copy-done.11 = f32[4,640]{1,0:T(4,128)} copy-done((f32[4,640]{1,0:T(4,128)}, f32[4,640]{1,0:T(4,128)S(1)}, u32[]{:S(2)}) %copy-start.11) | copy-done | bytes 10264
  42.7 0.7 %copy-done.8 = f32[4,640]{1,0:T(4,128)S(1)} copy-done((f32[4,640]{1,0:T(4,128)S(1)}, f32[4,640]{1,0:T(4,128)}, u32[]{:S(2)}) %copy-start.8) | copy-done | bytes 10264
  43.4 0.7 %copy-done.10 = f32[4,640]{1,0:T(4,128)S(1)} copy-done((f32[4,640]{1,0:T(4,128)S(1)}, f32[4,640]{1,0:T(4,128)}, u32[]{:S(2)}) %copy-start.10) | copy-done | bytes 10264
  44.1 0.7 %copy-done.12 = f32[4,640]{1,0:T(4,128)S(1)} copy-done((f32[4,640]{1,0:T(4,128)S(1)}, f32[4,640]{1,0:T(4,128)}, u32[]{:S(2)}) %copy-start.12) | copy-done | bytes 10264
  44.8 0.7 %copy-done.18 = s32[2]{0:T(128)S(1)} copy-done((s32[2]{0:T(128)S(1)}, s32[2]{0:T(128)}, u32[]{:S(2)}) %copy-start.18) | copy-done | bytes 32
  45.5 0.7 %copy-done.20 = f32[4]{0:T(128)S(1)} copy-done((f32[4]{0:T(128)S(1)}, f32[4]{0:T(128)}, u32[]{:S(2)}) %copy-start.20) | copy-done | bytes 40
  46.1 1.9 %legendre_back.1 = bf16[2,32,640]{2,1,0:T(8,128)(2,1)} custom-call(s32[2]{0:T(128)S(1)} %copy-done.18, f32[4]{0:T(128)S(1)} %copy-done.20, f32[4,640]{1,0:T(4,128)S(1)} %copy-done.12, f32[4,640]{1,0:T(4,128)S(1)} %copy-done.10, f32[4,640]{1,0:T(4,128)S(1)} %copy-done.8, bf16[2,32,640]{2,1,0:T(8,128)(2,1)S(1)} %copy-done.4, bf16[640,128]{1,0:T(8,128)(2,1)S(1)} %bitcast.4, ...), custom_call_target="tpu_custom_call" | custom-call | tf_op jit(solution)/shard_map/legendre_back/pallas_call | solution.py:444
  (32 shorter events, 0.1 us)
Async XLA Ops:
  0.0 18.5 %copy-start.14 = (f32[640]{0:T(1024)S(1)}, f32[640]{0:T(1024)}, u32[]{:S(2)}) copy-start(f32[640]{0:T(1024)} %constant.13.clone.refs_4_) | copy-start | bytes 7684
  0.0 1.9 %copy-start = (bf16[2,1280,640]{2,1,0:T(8,128)(2,1)S(1)}, bf16[2,1280,640]{2,1,0:T(8,128)(2,1)}, u32[]{:S(2)}) copy-start(bf16[2,1280,640]{2,1,0:T(8,128)(2,1)} %refs_8_.1) | copy-start | bytes 9830404
  1.9 0.9 %copy-start.3 = (bf16[2,32,640]{2,1,0:T(8,128)(2,1)S(1)}, bf16[2,32,640]{2,1,0:T(8,128)(2,1)}, u32[]{:S(2)}) copy-start(bf16[2,32,640]{2,1,0:T(8,128)(2,1)} %refs_5_.3) | copy-start | bytes 245764
  2.8 0.7 %copy-start.17 = (s32[2]{0:T(128)S(1)}, s32[2]{0:T(128)}, u32[]{:S(2)}) copy-start(s32[2]{0:T(128)} %refs_0_.3) | copy-start | bytes 28
  3.5 0.7 %copy-start.19 = (f32[4]{0:T(128)S(1)}, f32[4]{0:T(128)}, u32[]{:S(2)}) copy-start(f32[4]{0:T(128)} %refs_1_.4) | copy-start | bytes 52
  4.1 14.3 %copy-start.5 = (bf16[128,512]{1,0:T(8,128)(2,1)S(1)}, bf16[128,512]{1,0:T(8,128)(2,1)}, u32[]{:S(2)}) copy-start(bf16[128,512]{1,0:T(8,128)(2,1)} %constant.10.clone.refs_1_) | copy-start | bytes 393220
  4.1 14.3 %copy-start.13 = (f32[1280]{0:T(1024)S(1)}, f32[1280]{0:T(1024)}, u32[]{:S(2)}) copy-start(f32[1280]{0:T(1024)} %refs_5_.2) | copy-start | bytes 15364
  4.1 14.3 %copy-start.15 = (f32[640]{0:T(1024)S(1)}, f32[640]{0:T(1024)}, u32[]{:S(2)}) copy-start(f32[640]{0:T(1024)} %constant.12.clone.refs_3_) | copy-start | bytes 7684
  4.1 14.3 %copy-start.16 = (f32[8,128]{1,0:T(8,128)S(1)}, f32[8,128]{1,0:T(8,128)}, u32[]{:S(2)}) copy-start(f32[8,128]{1,0:T(8,128)} %constant.11.clone.refs_2_) | copy-start | bytes 12292
  4.2 38.5 %copy-start.1 = (bf16[2,1280,640]{2,1,0:T(8,128)(2,1)S(1)}, bf16[2,1280,640]{2,1,0:T(8,128)(2,1)}, u32[]{:S(2)}) copy-start(bf16[2,1280,640]{2,1,0:T(8,128)(2,1)} %refs_8_.1) | copy-start | bytes 9830404
  4.2 38.5 %copy-start.4 = (bf16[2,32,640]{2,1,0:T(8,128)(2,1)S(1)}, bf16[2,32,640]{2,1,0:T(8,128)(2,1)}, u32[]{:S(2)}) copy-start(bf16[2,32,640]{2,1,0:T(8,128)(2,1)} %refs_5_.3) | copy-start | bytes 245764
  4.2 38.5 %copy-start.6 = (bf16[128,128]{1,0:T(8,128)(2,1)S(1)}, bf16[128,128]{1,0:T(8,128)(2,1)}, u32[]{:S(2)}) copy-start(bf16[128,128]{1,0:T(8,128)(2,1)} %constant.14.clone.refs_7_) | copy-start | bytes 98308
  6.8 0.6 %copy-start.21 = (f32[4,640]{1,0:T(4,128)}, f32[4,640]{1,0:T(4,128)S(1)}, u32[]{:S(2)}) copy-start(f32[4,640]{1,0:T(4,128)S(1)} %get-tuple-element.7) | copy-start | bytes 30724
  29.3 0.7 %copy-start.2 = (bf16[640,128]{1,0:T(8,128)(2,1)}, bf16[640,128]{1,0:T(8,128)(2,1)S(1)}, u32[]{:S(2)}) copy-start(bf16[640,128]{1,0:T(8,128)(2,1)S(1)} %grid_stage.1) | copy-start | bytes 491524
  29.9 12.8 %all-to-all-start.1 = ((bf16[8,80,128]{2,1,0:T(8,128)(2,1)}), bf16[8,80,128]{2,1,0:T(8,128)(2,1)S(1)}, u32[]{:S(2)}, u32[]{:S(2)}) async-start(bf16[8,80,128]{2,1,0:T(8,128)(2,1)} %bitcast.5), calls=%async_computation.1 | async-start | bytes 327680 | tf_op jit(solution)/shard_map/all_to_all | solution.py:441
  33.3 7.6 %collective-permute-start.2 = (f32[4,640]{1,0:T(4,128)}, f32[4,640]{1,0:T(4,128)S(1)}, u32[]{:S(2)}, u32[]{:S(2)}) collective-permute-start(f32[4,640]{1,0:T(4,128)} %copy-done.21), channel_id=1, source_target_pairs={{3,0},{7,4},{11,8},{15,12},{19,16},{23,20},{27,24},{31,28}} | collective-permute-start | bytes 30728 | tf_op jit(solution)/shard_map/ppermute | solution.py:437
  34.6 6.9 %collective-permute-start.1 = (f32[4,640]{1,0:T(4,128)}, f32[4,640]{1,0:T(4,128)S(1)}, u32[]{:S(2)}, u32[]{:S(2)}) collective-permute-start(f32[4,640]{1,0:T(4,128)} %copy-done.21), channel_id=1, source_target_pairs={{2,0},{3,1},{6,4},{7,5},{10,8},{11,9},{14,12},{15,13},{18,16},{19,... | collective-permute-start | bytes 30728 | tf_op jit(solution)/shard_map/ppermute | solution.py:437
  35.9 6.2 %collective-permute-start = (f32[4,640]{1,0:T(4,128)}, f32[4,640]{1,0:T(4,128)S(1)}, u32[]{:S(2)}, u32[]{:S(2)}) collective-permute-start(f32[4,640]{1,0:T(4,128)} %copy-done.21), channel_id=1, source_target_pairs={{1,0},{2,1},{3,2},{5,4},{6,5},{7,6},{9,8},{10,9},{11,10},{13,12},{... | collective-permute-start | bytes 30728 | tf_op jit(solution)/shard_map/ppermute | solution.py:437
  42.1 0.6 %copy-start.11 = (f32[4,640]{1,0:T(4,128)}, f32[4,640]{1,0:T(4,128)S(1)}, u32[]{:S(2)}) copy-start(f32[4,640]{1,0:T(4,128)S(1)} %collective-permute-done.refs_2_) | copy-start | bytes 30724
  42.7 0.7 %copy-start.8 = (f32[4,640]{1,0:T(4,128)S(1)}, f32[4,640]{1,0:T(4,128)}, u32[]{:S(2)}) copy-start(f32[4,640]{1,0:T(4,128)} %copy-done.7) | copy-start | bytes 30724
  43.4 0.7 %copy-start.10 = (f32[4,640]{1,0:T(4,128)S(1)}, f32[4,640]{1,0:T(4,128)}, u32[]{:S(2)}) copy-start(f32[4,640]{1,0:T(4,128)} %copy-done.9) | copy-start | bytes 30724
  44.1 0.7 %copy-start.12 = (f32[4,640]{1,0:T(4,128)S(1)}, f32[4,640]{1,0:T(4,128)}, u32[]{:S(2)}) copy-start(f32[4,640]{1,0:T(4,128)} %copy-done.11) | copy-start | bytes 30724
  44.8 0.7 %copy-start.18 = (s32[2]{0:T(128)S(1)}, s32[2]{0:T(128)}, u32[]{:S(2)}) copy-start(s32[2]{0:T(128)} %refs_0_.3) | copy-start | bytes 28
  45.5 0.7 %copy-start.20 = (f32[4]{0:T(128)S(1)}, f32[4]{0:T(128)}, u32[]{:S(2)}) copy-start(f32[4]{0:T(128)} %refs_1_.4) | copy-start | bytes 52
  (2 other events, 1.2 us)
where the time goes:
time: 48.5 us; the launch traced here: 48 us
  Pallas kernels  15.3 us (32%)
  blocking collectives  11 us (23%)
  local copies, waits for them, and re-layouts  10.6 us (22%)
  starting transfers between devices  7.26 us (15%)
  waiting for transfers between devices  3.68 us (8%)
    all_to_all x1, blocking collectives, fast_body(): got = lax.all_to_all(sent, 'wave', split_axis=0, concat_axis=0, tiled=True)  11 us
    pallas_call x1, Pallas kernels, grid_call(): pl.pallas_call(lambda *refs: grid_kernel(n, *refs), out_shape=jax.ShapeDt...  10.8 us
    unnamed x44, local copies, waits for them, and re-layouts  10.6 us
    ppermute x3, starting transfers between devices, fast_body(): lax.ppermute(totals, 'lev', [(i, i - hop) for i in range(hop, n.n_lev)])  3.88 us
    ppermute x3, waiting for transfers between devices, fast_body(): lax.ppermute(totals, 'lev', [(i, i - hop) for i in range(hop, n.n_lev)])  3.68 us
    all_to_all x1, starting transfers between devices, fast_body(): lax.all_to_all(out.reshape(n.n_wave, n.rows, LANES), 'wave', split_axis=0...  3.38 us
    pallas_call x1, Pallas kernels, fast_body(): pl.pallas_call(lambda *refs: forward_kernel(n, *refs), out_shape=(jax.Sha...  2.65 us
    pallas_call x1, Pallas kernels, fast_body(): pl.pallas_call(lambda *refs: back_kernel(n, *refs), out_shape=jax.ShapeDt...  1.86 us
  transfers between devices with their start and end apart: 4, of which 1 were waited for; matrix products, arithmetic and copies ran while one was open for 0% of the time, Pallas kernels for 0%

commit v1 on v0

--- a/solution.py
+++ b/solution.py
@@ -15,7 +15,9 @@
 LANES = 128
 ROUNDER = 12582912.0
 CHUNK = 256
-GROUP = 4
+GROUP = 10
+PIECES = 2
+FLIGHT = 2
 
 
 def nt(a, b):
@@ -27,11 +29,11 @@
 
 
 def circle_polynomials():
-    f = np.cos(np.pi * (np.arange(4000) + 0.5) / 8000) * 0.5
+    f = np.cos(np.pi * (np.arange(4000) + 0.5) / 8000) * 0.505
     z = f * f
     out = []
-    for values, degree in ((np.cos(2 * np.pi * f), 6), (np.sin(2 * np.pi * f) / f, 6)):
-        fit = np.polynomial.chebyshev.Chebyshev.fit(z, values, degree, domain=[0, 0.25])
+    for values in (np.cos(np.pi * f), np.sin(np.pi * f) / f):
+        fit = np.polynomial.chebyshev.Chebyshev.fit(z, math.sqrt(2.0) * values, 4, domain=[0, 0.2551])
         out.append([float(c) for c in fit.convert(kind=np.polynomial.Polynomial).coef])
     return out
 
@@ -40,8 +42,8 @@
 
 
 def horner(z, coefs):
-    acc = jnp.full_like(z, coefs[-1])
-    for c in coefs[-2::-1]:
+    acc = z * coefs[-1] + coefs[-2]
+    for c in coefs[-3::-1]:
         acc = acc * z + c
     return acc
 
@@ -50,7 +52,8 @@
     turns = (count * inverse + ROUNDER) - ROUNDER
     f = (count - turns * length) * inverse
     z = f * f
-    return horner(z, COS_POLY), f * horner(z, SIN_POLY)
+    half_sin = f * horner(z, SIN_POLY)
+    return 1.0 - half_sin * half_sin, half_sin * horner(z, COS_POLY)
 
 
 def image_signs():
@@ -76,6 +79,7 @@
             and self.cols == 32
             and self.layers == 4
             and self.n_wave == 8
+            and self.n_lev == 4
             and self.rows % 16 == 0
             and self.half % (2 * GROUP) == 0
             and self.half % 8 == 0
@@ -91,19 +95,6 @@
             (h * owner, self.circles - h * (owner + 1)),
             (self.lats - h * (owner + 1), self.circles + h * owner),
         )
-
-
-def spread_matrix(n):
-    signs = image_signs()
-    out = np.zeros((LANES, 4 * LANES), np.float32)
-    for p in range(4):
-        for hemi in range(2):
-            for field in range(FIELDS):
-                for layer in range(n.layers):
-                    src = p * 32 + hemi * 16 + field * 4 + layer
-                    for image in range(IMAGES):
-                        out[src, p * LANES + image * 32 + field * 8 + hemi * 4 + layer] = signs[p, image]
-    return out
 
 
 def order_matrix(n):
@@ -146,24 +137,32 @@
     return copies
 
 
-def forward_kernel(n, wave_hbm, share_hbm, spec_hbm, leg_hbm, out_ref, total_hbm, wave_ref, share_ref, spec_ref, leg, total_ref, acc, sems, leg_sems, done_sem):
+def forward_kernel(n, wave_hbm, share_hbm, spec_hbm, leg_hbm, out_hbm, total_hbm, leg, high_hbm, wave_ref, share_ref, spec_ref, total_ref, high_ref, acc, sems, leg_sems, done_sems, out_ref, out_sems):
     small = fetch(((wave_hbm, wave_ref), (share_hbm, share_ref), (spec_hbm, spec_ref)), sems)
-    halves = [(s, hemi) for s in range(2) for hemi in range(2)]
-    big = fetch(
+    size = n.circles // PIECES
+    big = [
         [
-            (leg_hbm.at[s, pl.ds(hemi * n.circles, n.circles), :], leg.at[s, pl.ds(hemi * n.circles, n.circles), :])
-            for s, hemi in halves
-        ],
-        leg_sems,
-    )
+            pltpu.make_async_copy(leg_hbm.at[s, pl.ds(k * size, size), :], leg.at[s, pl.ds(k * size, size), :], leg_sems.at[s, k])
+            for s in range(2)
+        ]
+        for k in range(2 * PIECES)
+    ]
+    for pair in big[:FLIGHT]:
+        for copy in pair:
+            copy.start()
     for copy in small:
         copy.wait()
-    tables = []
+    row = lax.broadcasted_iota(jnp.int32, (n.cols, n.span), 0)
+    target = (row // n.layers) % FIELDS == 2
+    tables = [[], []]
     for s in range(2):
-        masked, _ = live_spec(n, spec_ref[s], wave_ref[s])
+        masked, live = live_spec(n, spec_ref[s], wave_ref[s])
         sums = layer_sums(n, masked, share_ref)
         for part in range(2):
             total_ref[2 * s + part : 2 * s + part + 1, :] = sums[part * 16 + 12 : part * 16 + 13, :]
+        high_ref[s] = jnp.where(target, pltpu.roll(sums, n.cols - n.layers, 0), 0.0)
+        leg[s, n.lats : n.lats + 8, :] = jnp.where(live[:8], 1.0, 0.0).astype(bf16)
+        leg[s, n.lats + 8 : n.lats + 16, :] = jnp.full((8, n.span), (1 - wave_ref[s] % 2).astype(f32)).astype(bf16)
         scaled = masked * jnp.where(wave_ref[s] == 0, 1.0, 2.0)
         none = jnp.zeros_like(scaled[:16])
         for hemi in range(2):
@@ -173,39 +172,71 @@
                 for part in range(2):
                     chunk = jnp.where(mine, scaled[part * 16 : part * 16 + 16], 0.0)
                     rows += [chunk, none] if hemi == 0 else [none, chunk]
-            tables.append(jnp.concatenate(rows, 0).astype(bf16))
-    totals_out = pltpu.make_async_copy(total_ref, total_hbm, done_sem)
-    totals_out.start()
-    for k, (s, hemi) in enumerate(halves):
-        big[k].wait()
-        piece = nt(leg[s, hemi * n.circles : (hemi + 1) * n.circles, :], tables[k])
-        acc[hemi] = piece if s == 0 else acc[hemi] + piece
+            tables[hemi].append(jnp.concatenate(rows, 0).astype(bf16))
+    tables = [jnp.concatenate(pair, 1) for pair in tables]
     even = jnp.where(wave_ref[0] % 2 == 0, wave_ref[0], wave_ref[1])
     lane = lax.broadcasted_iota(jnp.int32, (8, LANES), 1)
-    tag = jnp.where(lane < LANES // 2, even // 16, even % 16).astype(f32)
+    tag = jnp.where(lane < LANES // 2, even // 16, even % 16).astype(f32).astype(bf16)
     for owner in range(n.n_wave):
-        starts = n.block_starts(owner)
-        for b in range(2):
-            north = acc[0, starts[0][b] : starts[0][b] + n.half, :]
-            south = acc[1, starts[1][b] - n.circles : starts[1][b] - n.circles + n.half, :]
-            out_ref[owner, b * n.half : (b + 1) * n.half, :] = (north + south).astype(bf16)
-        out_ref[owner, n.rows : n.sent, :] = tag.astype(bf16)
-    totals_out.wait()
-
-
-def grid_kernel(n, got_ref, spread_ref, sign_ref, cor_ref, inv_ref, quad_ref, out_ref, spread, table_a, table_b, coef_a, coef_b, ret, rows):
+        out_ref[owner, n.rows : n.sent, :] = tag
+
+    def strip(start, count):
+        return out_ref.at[:, pl.ds(start, count), :], out_hbm.at[:, pl.ds(start, count), :]
+
+    leaving = fetch(((total_ref, total_hbm), (high_ref, high_hbm), strip(n.rows, 8)), done_sems)
+    for k in range(2 * PIECES):
+        for copy in big[k]:
+            copy.wait()
+        if k + FLIGHT < 2 * PIECES:
+            for copy in big[k + FLIGHT]:
+                copy.start()
+        rows = slice(k * size, (k + 1) * size)
+        both = jnp.concatenate([leg[0, rows, :], leg[1, rows, :]], 1)
+        acc[rows, :] = nt(both, tables[k // PIECES])
+        if k >= PIECES and (k + 1) % (PIECES // 2) == 0:
+            b = 3 - (k + 1) // (PIECES // 2) + 1
+            for owner in range(n.n_wave):
+                starts = n.block_starts(owner)
+                block = acc[starts[0][b] : starts[0][b] + n.half, :] + acc[starts[1][b] : starts[1][b] + n.half, :]
+                out_ref[owner, b * n.half : (b + 1) * n.half, :] = block.astype(bf16)
+            copy = pltpu.make_async_copy(*strip(b * n.half, n.half), out_sems.at[b])
+            copy.start()
+            leaving.append(copy)
+    for copy in leaving:
+        copy.wait()
+
+
+def grid_kernel(n, got_ref, sign_ref, near_ref, quad_hbm, total_hbm, out_hbm, pair_hbm, keep_hbm, spread, table_a, table_b, coef_a, coef_b, ret, rows, out, total_ref, pair_ref, keep_ref, quad_ref, out_sem, in_sems, side_sems, inv_ref, cor_ref):
+    arriving = fetch(((quad_hbm, quad_ref), (total_hbm, total_ref)), in_sems)
     device = lax.axis_index("wave")
     first_circle = device * n.half
     top = n.span - 1
-    for p in range(4):
-        spread[p] = nn(got_ref[...], spread_ref[:, p * LANES : (p + 1) * LANES])
     lane = lax.broadcasted_iota(jnp.int32, (8, LANES), 1)
     lane_f = lane.astype(f32)
     north = (lane // 4) % 2 == 0
+    sent_lane = lax.broadcasted_iota(jnp.int32, (LANES, LANES), 0)
+    to = lax.broadcasted_iota(jnp.int32, (LANES, LANES), 1)
+    source = (to // 4 % 2) * 16 + (to // 8 % FIELDS) * 4 + to % 4
+    for p in range(4):
+        pick = jnp.where(sent_lane == source + p * 32, sign_ref[p : p + 1, :], 0.0).astype(bf16)
+        wide = nn(got_ref[...], pick)
+        for src in range(n.n_wave):
+            for r in range(0, n.rows, 8):
+                spread[p, pl.ds(r * n.n_wave + src, 8, stride=n.n_wave), :] = wide[src * n.sent + r : src * n.sent + r + 8]
     raw = got_rows_f32(n, got_ref)
     tag = jnp.where(lane < LANES // 2, raw * 16.0, raw)
     even_m = tag + pltpu.roll(tag, LANES // 2, 1)
     odd_m = float(top) - even_m
+    even_2 = 2.0 * even_m
+    odd_2 = 2.0 * odd_m
+    for k in range(2):
+        step = lax.broadcasted_iota(jnp.int32, (n.half, LANES), 0)
+        circle = first_circle + step if k == 0 else n.circles - 1 - first_circle - step
+        inv_ref[k] = 1.0 / (20 + 4 * circle).astype(f32)
+        whole = jnp.full((n.half, LANES), 4.0 * n.lats, f32)
+        cosine, _ = cos_sin((2 * circle + 1).astype(f32), whole, 1.0 / (4 * n.lats))
+        cor_ref[k] = 2.0 * cosine
+    tile_point = (lax.broadcasted_iota(jnp.int32, (8, LANES), 0) * LANES + lane).astype(f32)
 
     def sizes(i):
         short = first_circle + i
@@ -216,27 +247,25 @@
         cut = (short + 6).astype(f32)
         len_s = (20 + 4 * short).astype(f32)
         len_l = (20 + 4 * long).astype(f32)
-        inv_s = inv_ref[short]
-        inv_l = inv_ref[long]
+        inv_s = inv_ref[0, pl.ds(i, 1), :]
+        inv_l = inv_ref[1, pl.ds(i, 1), :]
 
         def places(point):
             own = point < cut
-            return own, jnp.where(own, point, point - cut), jnp.where(own, len_s, len_l), jnp.where(own, inv_s, inv_l)
-
-        tile = lax.broadcasted_iota(jnp.int32, (8, LANES), 0)
-        _, j, length, inverse = places((tile * LANES + lane).astype(f32))
+            return jnp.where(own, point, point - cut), jnp.where(own, len_s, len_l), jnp.where(own, inv_s, inv_l)
+
+        j, length, inverse = places(tile_point)
         top_c, top_s = cos_sin(j * float(top), length, inverse)
         for t in range(n.tiles):
-            own, j, length, inverse = places(lane_f + float(t * LANES))
+            j, length, inverse = places(lane_f + float(t * LANES))
             c, s = cos_sin(even_m * j, length, inverse)
             tc = jnp.broadcast_to(top_c[t : t + 1, :], (8, LANES))
             ts = jnp.broadcast_to(top_s[t : t + 1, :], (8, LANES))
-            odd_c = tc * c + ts * s
-            odd_s = ts * c - tc * s
-            both = jnp.concatenate([c, s, odd_c, odd_s], 0)
-            own = jnp.concatenate([own] * 4, 0)
-            two = jnp.concatenate([jnp.where(own, both, 0.0), jnp.where(own, 0.0, both)], 0)
-            table[u, :, t * LANES : (t + 1) * LANES] = two.astype(bf16)
+            span = slice(t * LANES, (t + 1) * LANES)
+            table[u, 0:8, span] = c
+            table[u, 8:16, span] = s
+            table[u, 16:24, span] = tc * c + ts * s
+            table[u, 24:32, span] = ts * c - tc * s
 
     def gather(i, u, coef):
         short, long = sizes(i)
@@ -246,48 +275,68 @@
             (long, n.rows - 1 - i, n.half + i),
         ):
             length = (20 + 4 * circle).astype(f32)
-            even_ok = 2.0 * even_m < length
-            odd_ok = 2.0 * odd_m < length
             for p in range(4):
-                up = spread[p, pl.ds(row_n, 8, stride=n.sent), :]
-                down = spread[p, pl.ds(row_s, 8, stride=n.sent), :]
-                parts.append(jnp.where(odd_ok if p > 1 else even_ok, jnp.where(north, up, down), 0.0))
-        coef[u] = jnp.transpose(jnp.concatenate(parts, 0)).astype(bf16)
-
-    south = lax.broadcasted_iota(jnp.int32, (8, n.width), 0) // 4
-    point = lax.broadcasted_iota(jnp.int32, (8, n.width), 1)
-    point_row = lax.broadcasted_iota(jnp.int32, (1, n.width), 1)
+                up = spread[p, pl.ds(pl.multiple_of(row_n * 8, 8), 8), :]
+                down = spread[p, pl.ds(pl.multiple_of(row_s * 8, 8), 8), :]
+                seen = (odd_2 if p > 1 else even_2) < length
+                parts.append(jnp.where(seen, jnp.where(north, up, down), 0.0))
+        coef[u] = jnp.transpose(jnp.concatenate(parts, 0))
+
+    south = lax.broadcasted_iota(jnp.int32, (8, LANES), 0) // 4
+    lane_b = lax.broadcasted_iota(jnp.int32, (16, LANES), 1).astype(f32).astype(bf16)
     signs = [sign_ref[p : p + 1, :] for p in range(4)]
     group = lane // 32
     kinetic = jnp.where((lane // 8) % FIELDS == 2, 0.5, 1.0)
 
+    def weights(t, cut):
+        edge_at = jnp.clip(cut - t * LANES, -4, LANES + 4).astype(f32) - 0.5
+        x = jnp.full((16, LANES), edge_at, f32).astype(bf16) - lane_b
+        share = jnp.minimum(jnp.abs(x), 1.0)
+        own = jnp.minimum(jnp.maximum(x + 0.5, 0.0), 1.0)
+        if t == 0 or (t + 1) * LANES >= n.points:
+            point = lax.broadcasted_iota(jnp.int32, (16, LANES), 1) + t * LANES
+            ends = (point == 0) | (point == n.points - 1)
+            share = share * jnp.where(ends, 0.5, jnp.where(point < n.points, 1.0, 0.0)).astype(bf16)
+        own_share = own * share
+        return own, 1.0 - own, own_share, share - own_share
+
     def transform(i, u, table, coef):
         short, long = sizes(i)
         cut = short + 6
-        tab = table[u]
-        grid = nn(coef[u], tab).reshape(IMAGES, FIELDS, 8, n.width)
-        spin = jnp.where(point < cut, cor_ref[short], cor_ref[long])
-        spin = jnp.where(south == 0, spin, -spin)
-        x, y, curl, warm = grid[:, 0], grid[:, 1], grid[:, 2], grid[:, 3]
-        absolute = curl + spin
-        prods = jnp.stack([absolute * x, absolute * y, x * x + y * y, x * warm], 1)
-        prods = prods.reshape(LANES, n.width).astype(bf16)
-        edge = (point_row == 0) | (point_row == cut - 1) | (point_row == cut) | (point_row == n.points - 1)
-        share = jnp.where(edge, 0.5, jnp.where(point_row < n.points, 1.0, 0.0)).astype(bf16)
-        total = nt(tab * share, prods)
+        left = coef[u].astype(bf16)
+        cor_s = cor_ref[0, pl.ds(i, 1), :]
+        cor_l = cor_ref[1, pl.ds(i, 1), :]
+        total = None
+        for c in range(n.width // CHUNK):
+            ahead, behind, spins = [], [], []
+            for t in range(c * CHUNK // LANES, (c + 1) * CHUNK // LANES):
+                tab = table[u, :, t * LANES : (t + 1) * LANES].astype(bf16)
+                own, rest, own_share, rest_share = weights(t, cut)
+                ahead.append(jnp.concatenate([tab[:16] * own, tab[16:] * own, tab[:16] * rest, tab[16:] * rest], 0))
+                behind.append(
+                    jnp.concatenate(
+                        [tab[:16] * own_share, tab[16:] * own_share, tab[:16] * rest_share, tab[16:] * rest_share], 0
+                    )
+                )
+                spin = jnp.where(lane < cut - t * LANES, cor_s, cor_l)
+                spins.append(jnp.where(south == 0, spin, -spin))
+            grid = nn(left, jnp.concatenate(ahead, 1)).reshape(IMAGES, FIELDS, 8, CHUNK)
+            x, y, curl, warm = grid[:, 0], grid[:, 1], grid[:, 2], grid[:, 3]
+            absolute = curl + jnp.concatenate(spins, 1)
+            prods = jnp.stack([absolute * x, absolute * y, x * x + y * y, x * warm], 1)
+            piece = nt(jnp.concatenate(behind, 1), prods.reshape(LANES, CHUNK).astype(bf16))
+            total = piece if total is None else total + piece
         for k, circle in enumerate((short, long)):
             length = (20 + 4 * circle).astype(f32)
-            even_ok = 2.0 * even_m < length
-            odd_ok = 2.0 * odd_m < length
             folded = None
             for p in range(4):
                 y = total[(4 * k + p) * 8 : (4 * k + p + 1) * 8] * signs[p]
                 y = y + pltpu.roll(y, 64, 1)
                 y = y + pltpu.roll(y, 32, 1)
-                y = jnp.where(odd_ok if p > 1 else even_ok, y, 0.0)
+                y = jnp.where((odd_2 if p > 1 else even_2) < length, y, 0.0)
                 folded = y if folded is None else jnp.where(group == p, y, folded)
-            weight = jnp.where(north, quad_ref[circle], quad_ref[n.lats - 1 - circle]) * (inv_ref[circle] * kinetic)
-            ret[k, i] = folded * weight
+            weight = jnp.where(north, quad_ref[circle], quad_ref[n.lats - 1 - circle])
+            ret[k, i] = folded * (weight * (inv_ref[k, pl.ds(i, 1), :] * kinetic))
 
     def ready(start, table, coef):
         for u in range(GROUP):
@@ -308,6 +357,11 @@
         return carry
 
     ready(0, table_a, coef_a)
+    for copy in arriving:
+        copy.wait()
+    pair_ref[...] = total_ref[...] + near_ref[...]
+    keep_ref[...] = jnp.where(lax.axis_index("lev") % 2 == 0, near_ref[...], 0.0)
+    leaving = fetch(((pair_ref, pair_hbm), (keep_ref, keep_hbm)), side_sems)
     lax.fori_loop(0, n.half // (2 * GROUP), step, 0)
 
     def place(i, carry):
@@ -317,7 +371,12 @@
         return carry
 
     lax.fori_loop(0, n.half, place, 0, unroll=4)
-    out_ref[...] = rows[...].astype(bf16)
+    out[...] = rows[...].astype(bf16)
+    copy = pltpu.make_async_copy(out, out_hbm, out_sem)
+    copy.start()
+    for side in leaving:
+        side.wait()
+    copy.wait()
 
 
 def got_rows_f32(n, got_ref):
@@ -325,13 +384,8 @@
     return jnp.concatenate(pieces, 0)
 
 
-def back_kernel(n, wave_hbm, share_hbm, *refs):
-    deeper_hbm = refs[: n.n_lev - 1]
-    spec_ref, back_ref, order_ref, leg, out_ref, wave_ref, share_ref, deeper_ref, turn, sems = refs[n.n_lev - 1 :]
-    copies = fetch(
-        [(wave_hbm, wave_ref), (share_hbm, share_ref)] + [(ref, deeper_ref.at[k]) for k, ref in enumerate(deeper_hbm)],
-        sems,
-    )
+def back_kernel(n, far_hbm, keep_hbm, high_hbm, back_ref, order_ref, leg, out_ref, turn, far_ref, keep_ref, high_ref, sems):
+    arriving = fetch(((far_hbm, far_ref), (keep_hbm, keep_ref), (high_hbm, high_ref)), sems)
     for owner in range(n.n_wave):
         starts = n.block_starts(owner)
         for b in range(2):
@@ -342,23 +396,25 @@
     turned = [nt(order_ref[hemi * 64 : hemi * 64 + 64, :], turn[hemi]) for hemi in range(2)]
     row = lax.broadcasted_iota(jnp.int32, (n.cols, n.span), 0)
     target = (row // n.layers) % FIELDS == 2
-    for copy in copies:
+    sums = []
+    for s in range(2):
+        even = leg[s, n.lats + 8 : n.lats + 16, :].astype(f32)[:1] > 0.5
+        for hemi in range(2):
+            mine = jnp.where(even, turned[hemi][:32], turned[hemi][32:]).astype(bf16)
+            piece = nn(mine, leg[s, hemi * n.circles : (hemi + 1) * n.circles, :])
+            sums.append(piece if hemi == 0 else sums.pop() + piece)
+    for copy in arriving:
         copy.wait()
-    deeper = None
-    for k in range(n.n_lev - 1):
-        deeper = deeper_ref[k] if deeper is None else deeper + deeper_ref[k]
+    deeper = keep_ref[...] + jnp.where(lax.axis_index("lev") < n.n_lev // 2, far_ref[...], 0.0)
     for s in range(2):
-        masked, live = live_spec(n, spec_ref[s], wave_ref[s])
-        high = pltpu.roll(layer_sums(n, masked, share_ref), n.cols - n.layers, 0)
-        if deeper is not None:
-            low = jnp.where(row < 16, deeper[2 * s : 2 * s + 1], deeper[2 * s + 1 : 2 * s + 2])
-            high = high + low
-        even = wave_ref[s] % 2 == 0
-        tendency = jnp.where(target, high, 0.0)
-        for hemi in range(2):
-            mine = jnp.where(even, turned[hemi][:32], turned[hemi][32:])
-            tendency = tendency + nn(mine.astype(bf16), leg[s, hemi * n.circles : (hemi + 1) * n.circles, :])
+        live = leg[s, n.lats : n.lats + 8, :].astype(f32)[:1] > 0.5
+        low = jnp.where(row < 16, deeper[2 * s : 2 * s + 1], deeper[2 * s + 1 : 2 * s + 2])
+        tendency = sums[s] + high_ref[s] + jnp.where(target, low, 0.0)
         out_ref[s] = jnp.where(live, tendency, 0.0).astype(bf16)
+
+
+def stay(*arrays, space=pltpu.HBM):
+    return [pltpu.with_memory_space_constraint(x, space) for x in arrays]
 
 
 def smem():
@@ -373,37 +429,43 @@
     return pl.BlockSpec(memory_space=pltpu.HBM)
 
 
-def grid_call(n, got, quad_weight):
-    params = pltpu.CompilerParams(vmem_limit_bytes=24 * 1024 * 1024)
+def grid_call(n, got, quad_weight, totals, near):
     all_rows = n.n_wave * n.rows
-    circle = np.arange(n.circles)
-    spin = (2.0 * np.cos((circle + 0.5) * (math.pi / n.lats))).astype(np.float32)
-    inverse = (1.0 / (20 + 4 * circle)).astype(np.float32)
     signs = np.zeros((8, LANES), np.float32)
     signs[:4] = np.repeat(image_signs(), LANES // IMAGES, axis=1)
+    table = pltpu.VMEM((GROUP, n.keys // 2, n.width), f32)
+    coef = pltpu.VMEM((GROUP, LANES, n.keys), f32)
     return pl.pallas_call(
         lambda *refs: grid_kernel(n, *refs),
-        out_shape=jax.ShapeDtypeStruct((all_rows, LANES), bf16),
-        in_specs=[vmem(), vmem(), vmem(), smem(), smem(), smem()],
-        out_specs=vmem(),
+        out_shape=(pltpu.HBM((all_rows, LANES), bf16), pltpu.HBM(totals.shape, f32), pltpu.HBM(totals.shape, f32)),
+        in_specs=[vmem()] * 3 + [hbm()] * 2,
+        out_specs=(hbm(),) * 3,
         scratch_shapes=[
-            pltpu.VMEM((4, n.n_wave * n.sent, LANES), f32),
-            pltpu.VMEM((GROUP, n.keys, n.width), bf16),
-            pltpu.VMEM((GROUP, n.keys, n.width), bf16),
-            pltpu.VMEM((GROUP, LANES, n.keys), bf16),
-            pltpu.VMEM((GROUP, LANES, n.keys), bf16),
+            pltpu.VMEM((4, n.n_wave * n.rows, LANES), f32),
+            table,
+            table,
+            coef,
+            coef,
             pltpu.VMEM((2, n.half, 8, LANES), f32),
             pltpu.VMEM((all_rows, LANES), f32),
+            pltpu.VMEM((all_rows, LANES), bf16),
+            pltpu.VMEM(totals.shape, f32),
+            pltpu.VMEM(totals.shape, f32),
+            pltpu.VMEM(totals.shape, f32),
+            pltpu.SMEM((n.lats,), f32),
+            pltpu.SemaphoreType.DMA,
+            pltpu.SemaphoreType.DMA((2,)),
+            pltpu.SemaphoreType.DMA((2,)),
+            pltpu.VMEM((2, n.half, LANES), f32),
+            pltpu.VMEM((2, n.half, LANES), f32),
         ],
-        compiler_params=params,
+        compiler_params=pltpu.CompilerParams(vmem_limit_bytes=24 * 1024 * 1024),
         name="grid_stage",
     )(
         got,
-        jnp.asarray(spread_matrix(n), bf16),
         jnp.asarray(signs),
-        jnp.asarray(spin),
-        jnp.asarray(inverse),
-        quad_weight,
+        near,
+        *stay(quad_weight, totals),
     )
 
 
@@ -411,57 +473,61 @@
     params = pltpu.CompilerParams(vmem_limit_bytes=24 * 1024 * 1024)
     all_rows = n.n_wave * n.rows
     dma = pltpu.SemaphoreType.DMA
-    small = [pltpu.SMEM((2,), jnp.int32), pltpu.SMEM((n.layers,), f32)]
-    sent, totals = pl.pallas_call(
+    held_shape = (2, n.lats + 16, n.span)
+    high_shape = (2, n.cols, n.span)
+    total_shape = (4, n.span)
+    sent, totals, held, high = pl.pallas_call(
         lambda *refs: forward_kernel(n, *refs),
         out_shape=(
-            jax.ShapeDtypeStruct((n.n_wave, n.sent, LANES), bf16),
-            jax.ShapeDtypeStruct((4, n.span), f32),
+            pltpu.HBM((n.n_wave, n.sent, LANES), bf16),
+            pltpu.HBM(total_shape, f32),
+            pltpu.VMEM(held_shape, bf16),
+            pltpu.HBM(high_shape, f32),
         ),
         in_specs=[hbm()] * 4,
-        out_specs=(vmem(), hbm()),
-        scratch_shapes=small
-        + [
+        out_specs=(hbm(), hbm(), vmem(), hbm()),
+        scratch_shapes=[
+            pltpu.SMEM((2,), jnp.int32),
+            pltpu.SMEM((n.layers,), f32),
             pltpu.VMEM(spec.shape, bf16),
-            pltpu.VMEM(legendre.shape, bf16),
-            pltpu.VMEM((4, n.span), f32),
-            pltpu.VMEM((2, n.circles, LANES), f32),
+            pltpu.VMEM(total_shape, f32),
+            pltpu.VMEM(high_shape, f32),
+            pltpu.VMEM((n.lats, LANES), f32),
             dma((3,)),
-            dma((4,)),
-            dma,
+            dma((2, 2 * PIECES)),
+            dma((3,)),
+            pltpu.VMEM((n.n_wave, n.sent, LANES), bf16),
+            dma((2,)),
         ],
         compiler_params=params,
         name="legendre_forward",
-    )(wave_of_slot, layer_depth_share, spec, legendre)
-    deeper = [
-        lax.ppermute(totals, "lev", [(i, i - hop) for i in range(hop, n.n_lev)]) for hop in range(1, n.n_lev)
-    ]
+    )(*stay(wave_of_slot, layer_depth_share, spec, legendre))
+    near = lax.ppermute(totals, "lev", [(i, i ^ 1) for i in range(n.n_lev)])
     got = lax.all_to_all(sent, "wave", split_axis=0, concat_axis=0, tiled=True)
-    out = grid_call(n, got.reshape(n.n_wave * n.sent, LANES), quad_weight)
+    out, pair, keep = grid_call(n, got.reshape(n.n_wave * n.sent, LANES), quad_weight, totals, near)
+    far = lax.ppermute(pair, "lev", [(i, i ^ 2) for i in range(n.n_lev)])
     back = lax.all_to_all(
         out.reshape(n.n_wave, n.rows, LANES), "wave", split_axis=0, concat_axis=0, tiled=True
     )
     return pl.pallas_call(
         lambda *refs: back_kernel(n, *refs),
         out_shape=jax.ShapeDtypeStruct(spec.shape, bf16),
-        in_specs=[hbm()] * (n.n_lev + 1) + [vmem()] * 4,
+        in_specs=[hbm()] * 3 + [vmem()] * 3,
         out_specs=vmem(),
-        scratch_shapes=small
-        + [
-            pltpu.VMEM((max(n.n_lev - 1, 1), 4, n.span), f32),
+        scratch_shapes=[
             pltpu.VMEM((2, n.circles, LANES), bf16),
-            dma((n.n_lev + 1,)),
+            pltpu.VMEM(total_shape, f32),
+            pltpu.VMEM(total_shape, f32),
+            pltpu.VMEM(high_shape, f32),
+            dma((3,)),
         ],
         compiler_params=params,
         name="legendre_back",
     )(
-        wave_of_slot,
-        layer_depth_share,
-        *deeper,
-        spec,
+        *stay(far, keep, high),
         back.reshape(all_rows, LANES),
         jnp.asarray(order_matrix(n), bf16),
-        legendre,
+        *stay(held, space=pltpu.VMEM),
     )
 
 

time: 48.5 us -> 35.7 us (0.74)
  blocking collectives: 11 us -> 0 us
  local copies, waits for them, and re-layouts: 10.6 us -> 0.01 us
  starting transfers between devices: 7.26 us -> 12.8 us
  waiting for transfers between devices: 3.68 us -> 7.57 us
  Pallas kernels: 15.3 us -> 14.8 us
    all_to_all x1 -> x0, blocking collectives: 11 us -> none  [fast_body(): got = lax.all_to_all(sent, 'wave', split_axis=0, concat_axis=0, tiled=True)]
    unnamed x44 -> x6, local copies, waits for them, and re-layouts: 10.6 us -> 0.01 us
    all_to_all x0 -> x1, starting transfers between devices: none -> 5.21 us  [fast_body(): got = lax.all_to_all(sent, 'wave', split_axis=0, concat_axis=0, tiled=True)]
    all_to_all x0 -> x1, waiting for transfers between devices: none -> 2.14 us  [fast_body(): got = lax.all_to_all(sent, 'wave', split_axis=0, concat_axis=0, tiled=True)]
    all_to_all x1, waiting for transfers between devices: 0.01 us -> 0.94 us  [fast_body(): lax.all_to_all(out.reshape(n.n_wave, n.rows, LANES), 'wave', split_axis=0...]
    ppermute x3 -> x2, waiting for transfers between devices: 3.68 us -> 4.5 us  [the longest x1 2.31 us: fast_body(): near = lax.ppermute(totals, 'lev', [(i, i ^ 1) for i in range(n.n_lev)])]
    pallas_call x2, Pallas kernels: 13.4 us -> 12.8 us  [the longest x1 8.34 us: grid_call(): pl.pallas_call(lambda *refs: grid_kernel(n, *refs), out_shape=(pltpu.HBM(...]
    ppermute x3 -> x2, starting transfers between devices: 3.88 us -> 4.23 us  [the longest x1 2.66 us: fast_body(): far = lax.ppermute(pair, 'lev', [(i, i ^ 2) for i in range(n.n_lev)])]
  transfers between devices with their start and end apart: 4 -> 4, of which waited for: 1 -> 4; matrix products, arithmetic and copies ran while one was open for 0% -> 0% of each run, Pallas kernels for 0% -> 0%
where the time goes in v1:
time: 35.7 us; the launch traced here: 35.3 us
  Pallas kernels  14.8 us (41%)
  starting transfers between devices  12.8 us (36%)
  waiting for transfers between devices  7.57 us (21%)
    pallas_call x1, Pallas kernels, grid_call(): pl.pallas_call(lambda *refs: grid_kernel(n, *refs), out_shape=(pltpu.HBM(...  8.34 us
    all_to_all x1, starting transfers between devices, fast_body(): got = lax.all_to_all(sent, 'wave', split_axis=0, concat_axis=0, tiled=True)  5.21 us
    pallas_call x1, Pallas kernels, fast_body(): pl.pallas_call(lambda *refs: forward_kernel(n, *refs), out_shape=(pltpu.H...  4.49 us
    all_to_all x1, starting transfers between devices, fast_body(): lax.all_to_all(out.reshape(n.n_wave, n.rows, LANES), 'wave', split_axis=0...  3.39 us
    ppermute x1, starting transfers between devices, fast_body(): far = lax.ppermute(pair, 'lev', [(i, i ^ 2) for i in range(n.n_lev)])  2.66 us
    ppermute x1, waiting for transfers between devices, fast_body(): near = lax.ppermute(totals, 'lev', [(i, i ^ 1) for i in range(n.n_lev)])  2.31 us
    ppermute x1, waiting for transfers between devices, fast_body(): far = lax.ppermute(pair, 'lev', [(i, i ^ 2) for i in range(n.n_lev)])  2.19 us
    all_to_all x1, waiting for transfers between devices, fast_body(): got = lax.all_to_all(sent, 'wave', split_axis=0, concat_axis=0, tiled=True)  2.14 us
  transfers between devices with their start and end apart: 4, of which 4 were waited for; matrix products, arithmetic and copies ran while one was open for 0% of the time, Pallas kernels for 0%

profile of v1, /device:TPU:0, one launch (start us, length us, event | category | flops | bytes accessed | tf_op | source)
XLA Modules:
  0.0 35.3 jit_solution(4259337225113597226)
XLA Ops:
  0.0 0.0 copy-start.1
  0.0 0.0 copy-start
  0.0 4.5 %legendre_forward.1 = (bf16[8,88,128]{2,1,0:T(8,128)(2,1)}, f32[4,640]{1,0:T(4,128)}, bf16[2,1296,640]{2,1,0:T(8,128)(2,1)S(1)}, f32[2,32,640]{2,1,0:T(8,128)}) custom-call(s32[2]{0:T(128)} %refs_0_.1, f32[4]{0:T(128)} %refs_1_.2, bf16[2,32,640]{2,1,0:T(8,128)(2,1)} %refs_2_.1, bf16[2,1280,640]{2,1,0:T(8,128)(2,1)} %refs_3_.2), custom_call_target="tpu_custom_call" | custom-call | tf_op jit(solution)/shard_map/legendre_forward/pallas_call | solution.py:479
  4.5 5.2 %all-to-all-start = ((bf16[8,88,128]{2,1,0:T(8,128)(2,1)}), bf16[8,88,128]{2,1,0:T(8,128)(2,1)S(1)}, u32[]{:S(2)}, u32[]{:S(2)}) async-start(bf16[8,88,128]{2,1,0:T(8,128)(2,1)} %get-tuple-element.12), calls=%async_computation | async-start | bytes 360448 | tf_op jit(solution)/shard_map/all_to_all | solution.py:506
  9.7 1.6 %collective-permute-start = (f32[4,640]{1,0:T(4,128)}, f32[4,640]{1,0:T(4,128)S(1)}, u32[]{:S(2)}, u32[]{:S(2)}) collective-permute-start(f32[4,640]{1,0:T(4,128)} %get-tuple-element.13.refs_4_), channel_id=1, source_target_pairs={{0,1},{1,0},{2,3},{3,2},{4,5},{5,4},{6,7},{7,6},{8,9},{9,8},{10,11... | collective-permute-start | bytes 30728 | tf_op jit(solution)/shard_map/ppermute | solution.py:505
  11.3 2.3 %collective-permute-done.refs_2_ = f32[4,640]{1,0:T(4,128)S(1)} collective-permute-done((f32[4,640]{1,0:T(4,128)}, f32[4,640]{1,0:T(4,128)S(1)}, u32[]{:S(2)}, u32[]{:S(2)}) %collective-permute-start) | collective-permute-done | bytes 10272 | tf_op jit(solution)/shard_map/ppermute | solution.py:505
  13.6 2.1 %all-to-all-done = bf16[8,88,128]{2,1,0:T(8,128)(2,1)S(1)} async-done(((bf16[8,88,128]{2,1,0:T(8,128)(2,1)}), bf16[8,88,128]{2,1,0:T(8,128)(2,1)S(1)}, u32[]{:S(2)}, u32[]{:S(2)}) %all-to-all-start) | async-done | bytes 180256 | tf_op jit(solution)/shard_map/all_to_all | solution.py:506
  15.7 0.0 copy-done.1
  15.7 8.3 %grid_stage.1 = (bf16[640,128]{1,0:T(8,128)(2,1)}, f32[4,640]{1,0:T(4,128)}, f32[4,640]{1,0:T(4,128)}) custom-call(bf16[704,128]{1,0:T(8,128)(2,1)S(1)} %bitcast.3, f32[8,128]{1,0:T(8,128)S(1)} %copy-done.1, f32[4,640]{1,0:T(4,128)S(1)} %collective-permute-done.refs_2_, f32[1280]{0:T(1024)} %refs_3_.3, f32[4,640]{1,0:T(4,128)} %get-tuple-element.13.refs_4_), custom_call_target="tpu_custom_call" | custom-call | tf_op jit(solution)/shard_map/grid_stage/pallas_call | solution.py:438
  24.1 3.4 %all-to-all-start.1 = ((bf16[8,80,128]{2,1,0:T(8,128)(2,1)}), bf16[8,80,128]{2,1,0:T(8,128)(2,1)S(1)}, u32[]{:S(2)}, u32[]{:S(2)}) async-start(bf16[8,80,128]{2,1,0:T(8,128)(2,1)} %bitcast.5), calls=%async_computation.1 | async-start | bytes 327680 | tf_op jit(solution)/shard_map/all_to_all | solution.py:509
  27.5 2.7 %collective-permute-start.1 = (f32[4,640]{1,0:T(4,128)}, f32[4,640]{1,0:T(4,128)S(1)}, u32[]{:S(2)}, u32[]{:S(2)}) collective-permute-start(f32[4,640]{1,0:T(4,128)} %get-tuple-element.14), channel_id=1, source_target_pairs={{0,2},{1,3},{2,0},{3,1},{4,6},{5,7},{6,4},{7,5},{8,10},{9,11},{10,... | collective-permute-start | bytes 30728 | tf_op jit(solution)/shard_map/ppermute | solution.py:508
  30.2 2.2 %collective-permute-done.1.refs_0_ = f32[4,640]{1,0:T(4,128)S(1)} collective-permute-done((f32[4,640]{1,0:T(4,128)}, f32[4,640]{1,0:T(4,128)S(1)}, u32[]{:S(2)}, u32[]{:S(2)}) %collective-permute-start.1) | collective-permute-done | bytes 10272 | tf_op jit(solution)/shard_map/ppermute | solution.py:508
  32.3 0.0 copy-start.2
  32.3 0.9 %all-to-all-done.1 = bf16[8,80,128]{2,1,0:T(8,128)(2,1)S(1)} async-done(((bf16[8,80,128]{2,1,0:T(8,128)(2,1)}), bf16[8,80,128]{2,1,0:T(8,128)(2,1)S(1)}, u32[]{:S(2)}, u32[]{:S(2)}) %all-to-all-start.1) | async-done | bytes 163872 | tf_op jit(solution)/shard_map/all_to_all | solution.py:509
  33.3 0.0 copy-done.2
  33.3 0.0 copy-done
  33.3 2.0 %legendre_back.1 = bf16[2,32,640]{2,1,0:T(8,128)(2,1)} custom-call(f32[4,640]{1,0:T(4,128)} %copy-done.2, f32[4,640]{1,0:T(4,128)} %get-tuple-element.15.refs_1_, f32[2,32,640]{2,1,0:T(8,128)} %get-tuple-element.16.refs_2_, bf16[640,128]{1,0:T(8,128)(2,1)S(1)} %bitcast.4, bf16[128,128]{1,0:T(8,128)(2,1)S(1)} %copy-done, ...), custom_call_target="tpu_custom_call" | custom-call | tf_op jit(solution)/shard_map/legendre_back/pallas_call | solution.py:512
Async XLA Ops:
  0.0 15.7 %copy-start.1 = (f32[8,128]{1,0:T(8,128)S(1)}, f32[8,128]{1,0:T(8,128)}, u32[]{:S(2)}) copy-start(f32[8,128]{1,0:T(8,128)} %constant.4.clone.refs_1_) | copy-start | bytes 12292
  0.0 33.3 %copy-start = (bf16[128,128]{1,0:T(8,128)(2,1)S(1)}, bf16[128,128]{1,0:T(8,128)(2,1)}, u32[]{:S(2)}) copy-start(bf16[128,128]{1,0:T(8,128)(2,1)} %constant.5.clone.refs_4_) | copy-start | bytes 98308
  4.5 11.2 %all-to-all-start = ((bf16[8,88,128]{2,1,0:T(8,128)(2,1)}), bf16[8,88,128]{2,1,0:T(8,128)(2,1)S(1)}, u32[]{:S(2)}, u32[]{:S(2)}) async-start(bf16[8,88,128]{2,1,0:T(8,128)(2,1)} %get-tuple-element.12), calls=%async_computation | async-start | bytes 360448 | tf_op jit(solution)/shard_map/all_to_all | solution.py:506
  9.7 3.9 %collective-permute-start = (f32[4,640]{1,0:T(4,128)}, f32[4,640]{1,0:T(4,128)S(1)}, u32[]{:S(2)}, u32[]{:S(2)}) collective-permute-start(f32[4,640]{1,0:T(4,128)} %get-tuple-element.13.refs_4_), channel_id=1, source_target_pairs={{0,1},{1,0},{2,3},{3,2},{4,5},{5,4},{6,7},{7,6},{8,9},{9,8},{10,11... | collective-permute-start | bytes 30728 | tf_op jit(solution)/shard_map/ppermute | solution.py:505
  24.1 9.2 %all-to-all-start.1 = ((bf16[8,80,128]{2,1,0:T(8,128)(2,1)}), bf16[8,80,128]{2,1,0:T(8,128)(2,1)S(1)}, u32[]{:S(2)}, u32[]{:S(2)}) async-start(bf16[8,80,128]{2,1,0:T(8,128)(2,1)} %bitcast.5), calls=%async_computation.1 | async-start | bytes 327680 | tf_op jit(solution)/shard_map/all_to_all | solution.py:509
  27.5 4.8 %collective-permute-start.1 = (f32[4,640]{1,0:T(4,128)}, f32[4,640]{1,0:T(4,128)S(1)}, u32[]{:S(2)}, u32[]{:S(2)}) collective-permute-start(f32[4,640]{1,0:T(4,128)} %get-tuple-element.14), channel_id=1, source_target_pairs={{0,2},{1,3},{2,0},{3,1},{4,6},{5,7},{6,4},{7,5},{8,10},{9,11},{10,... | collective-permute-start | bytes 30728 | tf_op jit(solution)/shard_map/ppermute | solution.py:508
  32.3 0.9 %copy-start.2 = (f32[4,640]{1,0:T(4,128)}, f32[4,640]{1,0:T(4,128)S(1)}, u32[]{:S(2)}) copy-start(f32[4,640]{1,0:T(4,128)S(1)} %collective-permute-done.1.refs_0_) | copy-start | bytes 30724
